TPU v7x, 256 devices: a whole 4x4x8 slice. The times are simulated.
256 devices in a mesh: hot: 64 (over z, y, x_lo), cold: 4 (over x_hi, core).
Axes of the slice: x: 4 (x_hi: 2, x_lo: 2; x = x_hi * 2 + x_lo), y: 4, z: 8, core: 2. Of those that a mesh axis runs over, the one named last changes fastest.
Arguments:
- tokens: bfloat16 [64, 8192], replicated, may hold values from -6 to 6
- norm_gain: float32 [8192], replicated, may hold values from 0.1 to 1.9
- hot_gate: bfloat16 [4096, 8192], P(('hot', 'cold')), may hold values from -0.0625 to 0.0625
- hot_up: bfloat16 [4096, 8192], P(('hot', 'cold')), may hold values from -0.0625 to 0.0625
- hot_down: bfloat16 [4096, 8192], P(('hot', 'cold')), may hold values from -0.21875 to 0.21875
- hot_index: int32 [4096], replicated, may hold values from 0 to 14335, as said below
- cold_gate: bfloat16 [8192, 14336], P('hot', 'cold'), may hold values from -0.0625 to 0.0625
- cold_up: bfloat16 [8192, 14336], P('hot', 'cold'), may hold values from -0.0625 to 0.0625
- cold_down: bfloat16 [14336, 8192], P('cold', 'hot'), may hold values from -0.125 to 0.125
- block_mask: int32 [64, 112], P(None, 'cold'), may hold values from 0 to 1, as said below
Outputs:
- ffn_out: bfloat16 [64, 8192], P(None, ('hot', 'cold'))
Inputs may be any that keep to these rules, and one draw needn't show every extreme that they name: `hot_index`: distinct hidden units. `block_mask`: in each run of 28 blocks held by one index of cold, at most 14 blocks are active for any sequence, and some index reaches exactly 14.
All inputs are finite; a program needn't handle non-finite values.
Results may differ from a plain program's by a relative error of at most 0.0065.
Values may be sent and summed in bfloat16 or wider, within the bound.
A program may use at most 64 MiB of HBM per device.

v0:
```python
import jax
import jax.numpy as jnp
from jax import lax
from jax.sharding import Mesh
from jax.sharding import PartitionSpec as P

UNITS = 14336
COLD = ("cold_0", "cold_1")
HOT = ("hot_0", "hot_1", "hot_2")
HOT_COLD = ("hot_0", "hot_1", "hot_2", "cold_0", "cold_1")


def copy_for_each(x, axis):
    devices = lax.axis_size(axis)
    return lax.all_to_all(jnp.broadcast_to(x[None], (devices, *x.shape)), axis, 0, 0, tiled=True)


def joined_along(pieces, dim):
    shape = list(pieces.shape[1:])
    shape[dim] *= pieces.shape[0]
    return jnp.moveaxis(pieces, 0, dim).reshape(shape)


def collect(x, axis, dim):
    pieces = copy_for_each(x, axis)
    return joined_along(pieces, dim)


def all_blocks(x, axes, sequence):
    pieces = x
    for k in sequence:
        pieces = lax.all_gather(pieces, axes[k])
    done = sequence[::-1]
    back = [done.index(k) for k in range(len(axes))]
    pieces = pieces.transpose(*back, *range(len(axes), pieces.ndim))
    return pieces.reshape(-1, *x.shape)


def gathered_by_axis(x, axes, sequence, dim):
    return joined_along(all_blocks(x, axes, sequence), dim)


def cut_along(x, dim, devices):
    before, after = (x.shape[:dim], x.shape[dim + 1 :])
    return jnp.moveaxis(x.reshape(*before, devices, -1, *after), dim, 0)


def summed_on_arrival(x, axis, dim):
    pieces = cut_along(x, dim, lax.axis_size(axis))
    arrived = lax.all_to_all(pieces, axis, split_axis=0, concat_axis=0, tiled=True)
    return arrived.sum(axis=0)


def on_device(
    tokens,
    norm_gain,
    hot_gate,
    hot_up,
    hot_down,
    hot_index,
    cold_gate,
    cold_up,
    cold_down,
    block_mask,
):
    values = tokens.astype(jnp.float32)
    scale = lax.rsqrt(jnp.mean(values * values, axis=1, keepdims=True) + 1e-05)
    normed = (values * scale * norm_gain[None, :]).astype(jnp.bfloat16)
    dims = (((1,), (1,)), ((), ()))
    gate_hot = lax.dot_general(normed, hot_gate, dims, preferred_element_type=jnp.float32)
    up_hot = lax.dot_general(normed, hot_up, dims, preferred_element_type=jnp.float32)
    hidden_hot = (jax.nn.silu(gate_hot) * up_hot).astype(jnp.bfloat16)
    feat_rows = cold_gate.shape[0]
    unit_count = cold_gate.shape[1]
    out_cols = cold_down.shape[1]
    blocks_here = block_mask.shape[1]
    block = unit_count // blocks_here
    seqs = tokens.shape[0]
    is_hot = jnp.zeros((UNITS,), jnp.float32).at[hot_index].set(1.0)
    local_hot = lax.dynamic_slice_in_dim(is_hot, lax.axis_index(COLD) * unit_count, unit_count)
    capacity = blocks_here // 2
    positions = jnp.arange(blocks_here, dtype=jnp.int32)
    active = jnp.max(block_mask, axis=0) > 0
    slots = jnp.argsort(jnp.where(active, positions, positions + blocks_here))[:capacity]
    gate_w = cold_gate.reshape(feat_rows, blocks_here, block)[:, slots].reshape(
        feat_rows, capacity * block
    )
    up_w = cold_up.reshape(feat_rows, blocks_here, block)[:, slots].reshape(
        feat_rows, capacity * block
    )
    down_w = cold_down.reshape(blocks_here, block, out_cols)[slots].reshape(
        capacity * block, out_cols
    )
    seq_live = block_mask[:, slots].astype(jnp.float32)
    unit_live = 1.0 - local_hot.reshape(blocks_here, block)[slots]
    live = (seq_live[:, :, None] * unit_live[None, :, :]).reshape(seqs, capacity * block)
    gate_cols, up_cols = (
        lax.all_to_all(gate_w, HOT, split_axis=1, concat_axis=0, tiled=True),
        lax.all_to_all(up_w, HOT, split_axis=1, concat_axis=0, tiled=True),
    )
    gate_share = jnp.dot(normed, gate_cols, preferred_element_type=jnp.float32)
    up_share = jnp.dot(normed, up_cols, preferred_element_type=jnp.float32)
    share = gate_share.shape[1]
    live_share = lax.dynamic_slice_in_dim(live, lax.axis_index(HOT) * share, share, 1)
    piece = (jax.nn.silu(gate_share) * up_share * live_share).astype(jnp.bfloat16)
    hidden_cold = collect(piece, HOT, 1)
    out_cold = jnp.dot(hidden_cold, down_w, preferred_element_type=jnp.float32)
    down_cols = lax.all_to_all(hot_down, HOT_COLD, split_axis=1, concat_axis=0, tiled=True)
    hidden_all = gathered_by_axis(
        hidden_hot, (("hot_0", "hot_1", "hot_2", "cold_0"), "cold_1"), (0, 1), 1
    )
    hot_total = jnp.dot(hidden_all, down_cols, preferred_element_type=jnp.float32)
    cold_total = summed_on_arrival(out_cold, COLD, 1)
    total = hot_total + cold_total
    return total.astype(jnp.bfloat16)


def solution(mesh):
    split = Mesh(
        mesh.devices.reshape(8, 4, 2, 2, 2), ("hot_0", "hot_1", "hot_2", "cold_0", "cold_1")
    )
    placed = (
        P(),
        P(),
        P(HOT_COLD, None),
        P(HOT_COLD, None),
        P(HOT_COLD, None),
        P(),
        P(HOT, COLD),
        P(HOT, COLD),
        P(COLD, HOT),
        P(None, COLD),
    )
    return jax.shard_map(
        on_device, mesh=split, in_specs=placed, out_specs=P(None, HOT_COLD), check_vma=False
    )
```

profile of v0, /device:TPU:1, one launch (start us, length us, event | category | flops | bytes accessed | tf_op | source)
XLA Modules:
  0.0 460.4 jit_solution(4958017223762994111)
XLA Ops:
  0.0 0.9 reduce_max.9
  0.9 1.6 sort.17
  2.6 1.6 copy.32
  4.1 0.6 copy.33
  4.8 0.6 gather_fusion
  5.7 0.9 all_to_all.49
  6.6 13.6 %all-to-all-start.1 = ((bf16[128,64,28]{0,2,1:T(8,128)(2,1)}), bf16[128,64,28]{0,2,1:T(8,128)(2,1)S(1)}, u32[]{:S(2)}, u32[]{:S(2)}) async-start(bf16[128,64,28]{0,2,1:T(8,128)(2,1)} %all_to_all.49), calls=%async_computation.1 | async-start | bytes 1048576 | tf_op jit(solution)/shard_map/all_to_all | solution.py:98
  20.2 0.6 copy.36
  20.8 0.6 copy.37
  21.5 0.6 gather_fusion.1
  22.4 0.9 all_to_all.53
  23.3 15.5 %scatter_custom_fusion = f32[14336]{0:T(1024)S(1)} fusion(s32[4096]{0:T(1024)S(1)} %compare_select_fusion, f32[4096]{0:T(1024)S(1)} %broadcast.41, f32[]{:T(128)} %constant.17.clone.1), kind=kCustom, calls=%fused_computation.27 | custom fusion | bytes 57348 | tf_op jit(solution)/shard_map/scatter | solution.py:79
  38.9 10.9 %all-to-all-start.2 = ((bf16[128,64,28]{0,2,1:T(8,128)(2,1)}), bf16[128,64,28]{0,2,1:T(8,128)(2,1)}, u32[]{:S(2)}, u32[]{:S(2)}) async-start(bf16[128,64,28]{0,2,1:T(8,128)(2,1)} %all_to_all.53), calls=%async_computation.2 | async-start | bytes 1048576 | tf_op jit(solution)/shard_map/all_to_all | solution.py:99
  49.9 0.6 gather_fusion.2
  50.5 0.6 gather_fusion.3
  51.0 0.8 all_to_all.46
  51.8 0.7 copy.51
  52.5 1.4 reshape.134
  54.0 0.3 fusion
  54.6 0.3 copy.44
  54.9 9.8 %all-to-all-done.2 = bf16[128,64,28]{0,2,1:T(8,128)(2,1)} async-done(((bf16[128,64,28]{0,2,1:T(8,128)(2,1)}), bf16[128,64,28]{0,2,1:T(8,128)(2,1)}, u32[]{:S(2)}, u32[]{:S(2)}) %all-to-all-start.2) | async-done | bytes 458784 | tf_op jit(solution)/shard_map/all_to_all | solution.py:99
  64.7 1.2 copy.49
  66.0 0.3 copy.45
  66.4 0.3 copy-done.9
  66.7 0.5 fusion.15
  67.3 0.5 fusion.6
  67.8 1.0 reshape.130
  68.8 7.0 %all-to-all-start.3 = ((bf16[64,2,896]{2,1,0:T(2,128)(2,1)}), bf16[64,2,896]{2,1,0:T(2,128)(2,1)S(1)}, u32[]{:S(2)}, u32[]{:S(2)}) async-start(bf16[64,2,896]{2,1,0:T(2,128)(2,1)} %reshape.130), calls=%async_computation.3 | async-start | bytes 458752 | tf_op jit(solution)/shard_map/all_to_all | solution.py:15
  75.8 0.5 fusion.18
  76.2 0.5 copy-done.8
  76.7 0.5 fusion.8
  77.2 8.9 %all-to-all-done.3 = bf16[64,2,896]{2,1,0:T(2,128)(2,1)S(1)} async-done(((bf16[64,2,896]{2,1,0:T(2,128)(2,1)}), bf16[64,2,896]{2,1,0:T(2,128)(2,1)S(1)}, u32[]{:S(2)}, u32[]{:S(2)}) %all-to-all-start.3) | async-done | bytes 229408 | tf_op jit(solution)/shard_map/all_to_all | solution.py:15
  86.1 10.0 %all-to-all-start = ((bf16[256,2,256]{2,1,0:T(2,128)(2,1)}), bf16[256,2,256]{2,1,0:T(2,128)(2,1)S(1)}, u32[]{:S(2)}, u32[]{:S(2)}) async-start(bf16[256,2,256]{2,1,0:T(2,128)(2,1)} %reshape.134), calls=%async_computation | async-start | bytes 524288 | tf_op jit(solution)/shard_map/all_to_all | solution.py:108
  96.1 294.4 %all-gather.2 = bf16[128,64,16]{1,2,0:T(8,128)(2,1)S(1)} all-gather(bf16[1,64,16]{1,2,0:T(8,128)(2,1)S(1)} %fusion.8), channel_id=2, replica_groups=mesh['hot_0'=8,'hot_1'=4,'hot_2'=2,'cold_0'=2,'cold_1'=2] {'hot_0','hot_..., dimensions={0}, use_global_device_ids=true | all-gather | bytes 264192 | tf_op jit(solution)/shard_map/all_gather | solution.py:32
  390.5 0.8 gather_fusion.4
  391.5 0.6 copy.27
  392.1 0.3 reshape.131
  392.6 0.3 fusion.20
  392.9 0.7 reshape.132
  393.6 58.8 %all-to-all-start.4 = ((f32[4,1,2048]{2,1,0:T(1,128)}), f32[4,1,2048]{2,1,0:T(1,128)S(1)}, u32[]{:S(2)}, u32[]{:S(2)}) async-start(f32[4,1,2048]{2,1,0:T(1,128)} %reshape.132), calls=%async_computation.4 | async-start | bytes 65536 | tf_op jit(solution)/shard_map/all_to_all | solution.py:50
  452.4 2.2 all-gather.1
  454.8 1.2 copy.28
  456.0 0.8 copy.29
  456.9 0.5 reshape.135
  457.4 0.8 copy.31
  458.2 0.5 broadcast.58
  458.7 0.7 reduce
  459.6 0.9 fusion.5
  (45 shorter events, 1.9 us)
Async XLA Ops:
  0.0 390.5 %copy-start = (bf16[3584,128]{1,0:T(8,128)(2,1)S(1)}, bf16[3584,128]{1,0:T(8,128)(2,1)}, u32[]{:S(2)}) copy-start(bf16[3584,128]{1,0:T(8,128)(2,1)} %param.18) | copy-start | bytes 2752516
  2.6 47.9 %copy-start.6 = (s32[1024]{0:T(1024)}, s32[1024]{0:T(1024)S(1)}, u32[]{:S(2)}) copy-start(s32[1024]{0:T(1024)S(1)} %pad_clamp_fusion) | copy-start | bytes 12292
  5.7 14.5 %copy-start.3 = (bf16[128,3584]{1,0:T(8,128)(2,1)S(1)}, bf16[128,3584]{1,0:T(8,128)(2,1)}, u32[]{:S(2)}) copy-start(bf16[128,3584]{1,0:T(8,128)(2,1)} %param.17) | copy-start | bytes 2752516
  6.6 32.3 %all-to-all-start.1 = ((bf16[128,64,28]{0,2,1:T(8,128)(2,1)}), bf16[128,64,28]{0,2,1:T(8,128)(2,1)S(1)}, u32[]{:S(2)}, u32[]{:S(2)}) async-start(bf16[128,64,28]{0,2,1:T(8,128)(2,1)} %all_to_all.49), calls=%async_computation.1 | async-start | bytes 1048576 | tf_op jit(solution)/shard_map/all_to_all | solution.py:98
  22.1 1.2 copy-start.5
  22.4 27.5 %copy-start.1 = (s32[64,28]{0,1:T(8,128)S(1)}, s32[64,28]{0,1:T(8,128)}, u32[]{:S(2)}) copy-start(s32[64,28]{0,1:T(8,128)} %param.19) | copy-start | bytes 21508
  22.4 28.6 %copy-start.4 = (bf16[16,8192]{1,0:T(8,128)(2,1)S(1)}, bf16[16,8192]{1,0:T(8,128)(2,1)}, u32[]{:S(2)}) copy-start(bf16[16,8192]{1,0:T(8,128)(2,1)} %param.14) | copy-start | bytes 786436
  38.9 25.9 %all-to-all-start.2 = ((bf16[128,64,28]{0,2,1:T(8,128)(2,1)}), bf16[128,64,28]{0,2,1:T(8,128)(2,1)}, u32[]{:S(2)}, u32[]{:S(2)}) async-start(bf16[128,64,28]{0,2,1:T(8,128)(2,1)} %all_to_all.53), calls=%async_computation.2 | async-start | bytes 1048576 | tf_op jit(solution)/shard_map/all_to_all | solution.py:99
  52.5 1.5 copy-start.2
  65.9 0.8 copy-start.9
  67.7 8.0 %copy-start.7 = (bf16[16,8192]{1,0:T(8,128)(2,1)S(1)}, bf16[16,8192]{1,0:T(8,128)(2,1)}, u32[]{:S(2)}) copy-start(bf16[16,8192]{1,0:T(8,128)(2,1)} %param.12) | copy-start | bytes 786436
  68.8 17.3 %all-to-all-start.3 = ((bf16[64,2,896]{2,1,0:T(2,128)(2,1)}), bf16[64,2,896]{2,1,0:T(2,128)(2,1)S(1)}, u32[]{:S(2)}, u32[]{:S(2)}) async-start(bf16[64,2,896]{2,1,0:T(2,128)(2,1)} %reshape.130), calls=%async_computation.3 | async-start | bytes 458752 | tf_op jit(solution)/shard_map/all_to_all | solution.py:15
  75.8 1.0 copy-start.8
  86.1 307.5 %all-to-all-start = ((bf16[256,2,256]{2,1,0:T(2,128)(2,1)}), bf16[256,2,256]{2,1,0:T(2,128)(2,1)S(1)}, u32[]{:S(2)}, u32[]{:S(2)}) async-start(bf16[256,2,256]{2,1,0:T(2,128)(2,1)} %reshape.134), calls=%async_computation | async-start | bytes 524288 | tf_op jit(solution)/shard_map/all_to_all | solution.py:108
  393.6 64.6 %all-to-all-start.4 = ((f32[4,1,2048]{2,1,0:T(1,128)}), f32[4,1,2048]{2,1,0:T(1,128)S(1)}, u32[]{:S(2)}, u32[]{:S(2)}) async-start(f32[4,1,2048]{2,1,0:T(1,128)} %reshape.132), calls=%async_computation.4 | async-start | bytes 65536 | tf_op jit(solution)/shard_map/all_to_all | solution.py:50
where the time goes:
time: 461 us; the launch traced here: 460 us
  blocking collectives  297 us (64%)
  starting transfers between devices  100 us (22%)
  local copies, waits for them, and re-layouts  37.9 us (8%)
  waiting for transfers between devices  18.7 us (4%)
    all_gather x2, blocking collectives, all_blocks(): pieces = lax.all_gather(pieces, axes[k])  297 us
    all_to_all x1, starting transfers between devices, summed_on_arrival(): lax.all_to_all(pieces, axis, split_axis=0, concat_axis=0, tiled=True)  58.8 us
    scatter x1, local copies, waits for them, and re-layouts, on_device(): is_hot = jnp.zeros((UNITS,), jnp.float32).at[hot_index].set(1.0)  15.5 us
    all_to_all x1, starting transfers between devices, on_device(): lax.all_to_all(gate_w, HOT, split_axis=1, concat_axis=0, tiled=True)  13.6 us
    all_to_all x1, starting transfers between devices, on_device(): lax.all_to_all(up_w, HOT, split_axis=1, concat_axis=0, tiled=True)  10.9 us
    all_to_all x1, starting transfers between devices, on_device(): lax.all_to_all(hot_down, HOT_COLD, split_axis=1, concat_axis=0, tiled=True)  9.98 us
    all_to_all x1, waiting for transfers between devices, on_device(): lax.all_to_all(up_w, HOT, split_axis=1, concat_axis=0, tiled=True)  9.79 us
  transfers between devices with their start and end apart: 5, of which 2 were waited for; matrix products, arithmetic and copies ran while one was open for 6% of the time, Pallas kernels for 0%

commit v1 on v0

--- a/solution.py
+++ b/solution.py
@@ -63,6 +63,18 @@
     cold_down,
     block_mask,
 ):
+
+    def _plan_shards(x_part):
+        return jnp.concatenate(
+            lax.all_to_all(
+                jnp.stack(jnp.split(x_part, lax.axis_size(HOT_COLD), axis=1), axis=0),
+                concat_axis=0,
+                axis_name=HOT_COLD,
+                split_axis=0,
+            ),
+            axis=0,
+        )
+
     values = tokens.astype(jnp.float32)
     scale = lax.rsqrt(jnp.mean(values * values, axis=1, keepdims=True) + 1e-05)
     normed = (values * scale * norm_gain[None, :]).astype(jnp.bfloat16)
@@ -105,7 +117,7 @@
     piece = (jax.nn.silu(gate_share) * up_share * live_share).astype(jnp.bfloat16)
     hidden_cold = collect(piece, HOT, 1)
     out_cold = jnp.dot(hidden_cold, down_w, preferred_element_type=jnp.float32)
-    down_cols = lax.all_to_all(hot_down, HOT_COLD, split_axis=1, concat_axis=0, tiled=True)
+    down_cols = _plan_shards(hot_down)
     hidden_all = gathered_by_axis(
         hidden_hot, (("hot_0", "hot_1", "hot_2", "cold_0"), "cold_1"), (0, 1), 1
     )

time: 461 us -> 625 us (1.36)
  local copies, waits for them, and re-layouts: 37.9 us -> 203 us
    unnamed x33 -> x290, local copies, waits for them, and re-layouts: 7.92 us -> 175 us
  transfers between devices with their start and end apart: 5 -> 5, of which waited for: 2 -> 2; matrix products, arithmetic and copies ran while one was open for 6% -> 31% of each run, Pallas kernels for 0% -> 0%
where the time goes in v1:
time: 625 us
  blocking collectives  297 us (48%)
  local copies, waits for them, and re-layouts  203 us (32%)
  starting transfers between devices  100 us (16%)
  waiting for transfers between devices  17.5 us (3%)
    all_gather x2, blocking collectives, all_blocks(): pieces = lax.all_gather(pieces, axes[k])  297 us
    unnamed x290, local copies, waits for them, and re-layouts  175 us
    all_to_all x1, starting transfers between devices, summed_on_arrival(): lax.all_to_all(pieces, axis, split_axis=0, concat_axis=0, tiled=True)  58.8 us
    scatter x1, local copies, waits for them, and re-layouts, on_device(): is_hot = jnp.zeros((UNITS,), jnp.float32).at[hot_index].set(1.0)  15.5 us
    all_to_all x1, starting transfers between devices, on_device(): lax.all_to_all(gate_w, HOT, split_axis=1, concat_axis=0, tiled=True)  13.6 us
  transfers between devices with their start and end apart: 5, of which 2 were waited for; matrix products, arithmetic and copies ran while one was open for 31% of the time, Pallas kernels for 0%

profile of v1, /device:TPU:1, one launch (start us, length us, event | category | flops | bytes accessed | tf_op | source)
XLA Modules:
  0.0 624.6 jit_solution(11862046659761710514)
XLA Ops:
  0.0 0.9 reduce_max.9
  0.9 1.6 sort.17
  2.6 1.6 copy.571
  5.7 0.9 all_to_all.38
  6.6 13.6 %all-to-all-start.1 = ((bf16[128,64,28]{0,2,1:T(8,128)(2,1)}), bf16[128,64,28]{0,2,1:T(8,128)(2,1)S(1)}, u32[]{:S(2)}, u32[]{:S(2)}) async-start(bf16[128,64,28]{0,2,1:T(8,128)(2,1)} %all_to_all.38), calls=%async_computation.1 | async-start | bytes 1048576 | tf_op jit(solution)/shard_map/all_to_all | solution.py:110
  24.1 0.7 constant_dynamic-update-slice_fusion.249
  26.7 0.7 constant_dynamic-update-slice_fusion.245
  33.8 0.7 constant_dynamic-update-slice_fusion.234
  50.6 0.7 constant_dynamic-update-slice_fusion.208
  57.1 0.7 constant_dynamic-update-slice_fusion.198
  60.3 0.7 constant_dynamic-update-slice_fusion.193
  71.3 0.7 constant_dynamic-update-slice_fusion.176
  75.2 0.7 constant_dynamic-update-slice_fusion.170
  84.3 0.7 constant_dynamic-update-slice_fusion.156
  94.6 0.7 constant_dynamic-update-slice_fusion.140
  107.5 0.7 constant_dynamic-update-slice_fusion.120
  112.7 0.7 constant_dynamic-update-slice_fusion.112
  132.0 0.7 constant_dynamic-update-slice_fusion.82
  142.3 0.7 constant_dynamic-update-slice_fusion.66
  145.6 0.7 constant_dynamic-update-slice_fusion.61
  161.1 0.7 constant_dynamic-update-slice_fusion.37
  169.5 0.7 constant_dynamic-update-slice_fusion.24
  174.0 0.7 constant_dynamic-update-slice_fusion.17
  176.6 0.7 constant_dynamic-update-slice_fusion.13
  179.9 0.7 constant_dynamic-update-slice_fusion.8
  181.1 0.7 constant_dynamic-update-slice_fusion.6
  184.4 0.8 gather_fusion.1
  185.4 0.9 all_to_all.42
  186.3 15.5 %scatter_custom_fusion = f32[14336]{0:T(1024)S(1)} fusion(s32[4096]{0:T(1024)S(1)} %compare_select_fusion, f32[4096]{0:T(1024)S(1)} %broadcast.41, f32[]{:T(128)} %constant.17.clone.1), kind=kCustom, calls=%fused_computation.283 | custom fusion | bytes 57348 | tf_op jit(solution)/shard_map/scatter | solution.py:91
  204.5 10.8 %all-to-all-start.2 = ((bf16[128,64,28]{0,2,1:T(8,128)(2,1)}), bf16[128,64,28]{0,2,1:T(8,128)(2,1)S(1)}, u32[]{:S(2)}, u32[]{:S(2)}) async-start(bf16[128,64,28]{0,2,1:T(8,128)(2,1)} %all_to_all.42), calls=%async_computation.2 | async-start | bytes 1048576 | tf_op jit(solution)/shard_map/all_to_all | solution.py:111
  215.4 0.8 gather_fusion.2
  216.2 0.7 gather_fusion.3
  216.9 2.9 reshape.132
  220.5 1.1 copy.583
  221.6 8.6 %all-to-all-done.2 = bf16[128,64,28]{0,2,1:T(8,128)(2,1)S(1)} async-done(((bf16[128,64,28]{0,2,1:T(8,128)(2,1)}), bf16[128,64,28]{0,2,1:T(8,128)(2,1)S(1)}, u32[]{:S(2)}, u32[]{:S(2)}) %all-to-all-start.2) | async-done | bytes 458784 | tf_op jit(solution)/shard_map/all_to_all | solution.py:111
  232.6 1.0 reshape.128
  233.6 7.0 %all-to-all-start.3 = ((bf16[64,2,896]{2,1,0:T(2,128)(2,1)}), bf16[64,2,896]{2,1,0:T(2,128)(2,1)S(1)}, u32[]{:S(2)}, u32[]{:S(2)}) async-start(bf16[64,2,896]{2,1,0:T(2,128)(2,1)} %reshape.128), calls=%async_computation.3 | async-start | bytes 458752 | tf_op jit(solution)/shard_map/all_to_all | solution.py:15
  242.0 8.9 %all-to-all-done.3 = bf16[64,2,896]{2,1,0:T(2,128)(2,1)S(1)} async-done(((bf16[64,2,896]{2,1,0:T(2,128)(2,1)}), bf16[64,2,896]{2,1,0:T(2,128)(2,1)S(1)}, u32[]{:S(2)}, u32[]{:S(2)}) %all-to-all-start.3) | async-done | bytes 229408 | tf_op jit(solution)/shard_map/all_to_all | solution.py:15
  250.9 10.0 %all-to-all-start = ((bf16[256,2,256]{2,1,0:T(2,128)(2,1)}), bf16[256,2,256]{2,1,0:T(2,128)(2,1)S(1)}, u32[]{:S(2)}, u32[]{:S(2)}) async-start(bf16[256,2,256]{2,1,0:T(2,128)(2,1)} %reshape.132), calls=%async_computation | async-start | bytes 524288 | tf_op jit(solution)/shard_map/all_to_all | solution.py:69
  260.8 294.4 %all-gather.2 = bf16[128,64,16]{1,2,0:T(8,128)(2,1)S(1)} all-gather(bf16[1,64,16]{1,2,0:T(8,128)(2,1)S(1)} %fusion.8), channel_id=2, replica_groups=mesh['hot_0'=8,'hot_1'=4,'hot_2'=2,'cold_0'=2,'cold_1'=2] {'hot_0','hot_..., dimensions={0}, use_global_device_ids=true | all-gather | bytes 264192 | tf_op jit(solution)/shard_map/all_gather | solution.py:32
  555.3 0.8 gather_fusion.4
  557.7 0.7 reshape.130
  558.4 58.8 %all-to-all-start.4 = ((f32[4,1,2048]{2,1,0:T(1,128)}), f32[4,1,2048]{2,1,0:T(1,128)S(1)}, u32[]{:S(2)}, u32[]{:S(2)}) async-start(f32[4,1,2048]{2,1,0:T(1,128)} %reshape.130), calls=%async_computation.4 | async-start | bytes 65536 | tf_op jit(solution)/shard_map/all_to_all | solution.py:50
  617.2 2.2 all-gather.1
  619.5 1.2 copy.568
  620.8 0.8 copy.569
  622.7 0.7 reduce
  623.5 1.1 fusion.5
  (300 shorter events, 161.7 us)
Async XLA Ops:
  0.0 555.3 %copy-start = (bf16[3584,128]{1,0:T(8,128)(2,1)S(1)}, bf16[3584,128]{1,0:T(8,128)(2,1)}, u32[]{:S(2)}) copy-start(bf16[3584,128]{1,0:T(8,128)(2,1)} %param.18) | copy-start | bytes 2752516
  2.6 4.1 copy-start.7
  5.7 14.5 %copy-start.6 = (s32[4096]{0:T(1024)S(1)}, s32[4096]{0:T(1024)}, u32[]{:S(2)}) copy-start(s32[4096]{0:T(1024)} %param.15) | copy-start | bytes 49156
  5.7 14.5 %copy-start.2 = (bf16[16,8192]{1,0:T(8,128)(2,1)S(1)}, bf16[16,8192]{1,0:T(8,128)(2,1)}, u32[]{:S(2)}) copy-start(bf16[16,8192]{1,0:T(8,128)(2,1)} %param.14) | copy-start | bytes 786436
  6.6 197.9 %all-to-all-start.1 = ((bf16[128,64,28]{0,2,1:T(8,128)(2,1)}), bf16[128,64,28]{0,2,1:T(8,128)(2,1)S(1)}, u32[]{:S(2)}, u32[]{:S(2)}) async-start(bf16[128,64,28]{0,2,1:T(8,128)(2,1)} %all_to_all.38), calls=%async_computation.1 | async-start | bytes 1048576 | tf_op jit(solution)/shard_map/all_to_all | solution.py:110
  20.2 162.9 %copy-start.4 = (bf16[128,3584]{1,0:T(8,128)(2,1)S(1)}, bf16[128,3584]{1,0:T(8,128)(2,1)}, u32[]{:S(2)}) copy-start(bf16[128,3584]{1,0:T(8,128)(2,1)} %param.17) | copy-start | bytes 2752516
  185.4 30.0 %copy-start.1 = (s32[64,28]{0,1:T(8,128)S(1)}, s32[64,28]{0,1:T(8,128)}, u32[]{:S(2)}) copy-start(s32[64,28]{0,1:T(8,128)} %param.19) | copy-start | bytes 21508
  204.5 25.7 %all-to-all-start.2 = ((bf16[128,64,28]{0,2,1:T(8,128)(2,1)}), bf16[128,64,28]{0,2,1:T(8,128)(2,1)S(1)}, u32[]{:S(2)}, u32[]{:S(2)}) async-start(bf16[128,64,28]{0,2,1:T(8,128)(2,1)} %all_to_all.42), calls=%async_computation.2 | async-start | bytes 1048576 | tf_op jit(solution)/shard_map/all_to_all | solution.py:111
  215.3 4.6 copy-start.3
  230.4 1.0 copy-start.5
  230.4 1.0 copy-start.10
  232.5 8.0 %copy-start.8 = (bf16[16,8192]{1,0:T(8,128)(2,1)S(1)}, bf16[16,8192]{1,0:T(8,128)(2,1)}, u32[]{:S(2)}) copy-start(bf16[16,8192]{1,0:T(8,128)(2,1)} %param.12) | copy-start | bytes 786436
  233.6 17.3 %all-to-all-start.3 = ((bf16[64,2,896]{2,1,0:T(2,128)(2,1)}), bf16[64,2,896]{2,1,0:T(2,128)(2,1)S(1)}, u32[]{:S(2)}, u32[]{:S(2)}) async-start(bf16[64,2,896]{2,1,0:T(2,128)(2,1)} %reshape.128), calls=%async_computation.3 | async-start | bytes 458752 | tf_op jit(solution)/shard_map/all_to_all | solution.py:15
  240.5 1.0 copy-start.9
  250.9 307.5 %all-to-all-start = ((bf16[256,2,256]{2,1,0:T(2,128)(2,1)}), bf16[256,2,256]{2,1,0:T(2,128)(2,1)S(1)}, u32[]{:S(2)}, u32[]{:S(2)}) async-start(bf16[256,2,256]{2,1,0:T(2,128)(2,1)} %reshape.132), calls=%async_computation | async-start | bytes 524288 | tf_op jit(solution)/shard_map/all_to_all | solution.py:69
  558.4 63.8 %all-to-all-start.4 = ((f32[4,1,2048]{2,1,0:T(1,128)}), f32[4,1,2048]{2,1,0:T(1,128)S(1)}, u32[]{:S(2)}, u32[]{:S(2)}) async-start(f32[4,1,2048]{2,1,0:T(1,128)} %reshape.130), calls=%async_computation.4 | async-start | bytes 65536 | tf_op jit(solution)/shard_map/all_to_all | solution.py:50
